TPU v7x, 32 devices: a whole 2x2x4 slice. The times are simulated.
32 devices in a mesh: seq: 8 (over z, y), head: 4 (over x, core).
Axes of the slice: x: 2, y: 2, z: 4, core: 2. Of those that a mesh axis runs over, the one named last changes fastest.
Arguments:
- queries: bfloat16 [4096, 2048], P('seq', 'head'), may hold values from -6 to 6
- key_vectors: bfloat16 [4096, 2048], P('seq', 'head'), may hold values from -6 to 6
- value_vectors: bfloat16 [4096, 2048], P('seq', 'head'), may hold values from -6 to 6
- gate_input: bfloat16 [4096, 2048], P('seq', 'head'), may hold values from -6 to 6
- out_weight: bfloat16 [2048, 4096], P('seq', 'head'), may hold values from -0.125 to 0.125
Outputs:
- layer_output: bfloat16 [4096, 4096], P('seq', 'head')
All inputs are finite; a program needn't handle non-finite values.
Results may differ from a plain program's by a relative error of at most 0.0057.
Values may be sent and summed in bfloat16 or wider, within the bound.
A program may use at most 64 MiB of HBM per device.

v0:
```python
import jax
import jax.numpy as jnp
from jax import lax
from jax.sharding import PartitionSpec as P

HD = 128


def carried_in(shard, axis, combine, identity):
    count, position = (lax.axis_size(axis), lax.axis_index(axis))
    everything = lax.all_gather(shard, axis)
    start = jnp.broadcast_to(jnp.asarray(identity, shard.dtype), shard.shape)

    def turn(k, before):
        reached = k < position
        new = combine(before, everything[k])
        return jnp.where(reached, new, before)

    return lax.fori_loop(0, count, turn, start)


def add_states(earlier, later):
    return earlier + later


def carried(own_state):
    return carried_in(own_state, "seq", add_states, jnp.zeros_like(own_state))


def in_shard(qhead, khead, vhead, scale):
    rows = qhead.shape[0]
    step = min(rows, 512)
    scores = jnp.einsum("thd,shd->hts", qhead, khead, preferred_element_type=jnp.float32) * scale
    rowpos = 0 + lax.broadcasted_iota(jnp.int32, (step, step), 0)
    colpos = lax.broadcasted_iota(jnp.int32, (step, step), 1)
    scores = jnp.where((colpos <= rowpos)[None, :, :], scores, 0.0).astype(jnp.bfloat16)
    pieces = jnp.einsum("hts,she->the", scores, vhead, preferred_element_type=jnp.float32)
    return pieces


def per_device(queries, key_vectors, value_vectors, gate_input, out_weight):
    rows, width = queries.shape
    heads = width // HD
    scale = HD ** (-0.5)
    qhead = queries.reshape(rows, heads, HD)
    khead = key_vectors.reshape(rows, heads, HD)
    vhead = value_vectors.reshape(rows, heads, HD)
    own_state = jnp.einsum("thd,the->hde", khead, vhead, preferred_element_type=jnp.float32)
    local = in_shard(qhead, khead, vhead, scale)
    prefix = carried(own_state)
    inter = (
        jnp.einsum(
            "thd,hde->the", qhead, prefix.astype(jnp.bfloat16), preferred_element_type=jnp.float32
        )
        * scale
    )
    attn = (local + inter).reshape(rows, width)
    squares = jnp.sum(attn * attn, axis=1)
    hidden = (attn * jax.nn.silu(gate_input.astype(jnp.float32))).astype(jnp.bfloat16)
    total = lax.psum(squares, "head")
    features = lax.all_gather(hidden, "head", axis=1, tiled=True)
    full_block = lax.all_gather(out_weight, "seq", axis=0, tiled=True)
    projected = jnp.dot(features, full_block, preferred_element_type=jnp.float32)
    mean_square = total / features.shape[1]
    return (projected * lax.rsqrt(mean_square + 1e-06)[:, None]).astype(jnp.bfloat16)


def solution(mesh):
    placed = (
        P("seq", "head"),
        P("seq", "head"),
        P("seq", "head"),
        P("seq", "head"),
        P("seq", "head"),
    )
    return jax.shard_map(
        per_device, mesh=mesh, in_specs=placed, out_specs=P("seq", "head"), check_vma=False
    )
```

profile of v0, /device:TPU:0, one launch (start us, length us, event | category | flops | bytes accessed | tf_op | source)
XLA Modules:
  0.0 184.2 jit_solution(1914398323355310470)
XLA Ops:
  6.5 0.0 copy-start
  6.5 0.0 all-gather.9.cloned.1.call-start
  6.5 1.3 copy.19
  7.9 2.0 %fusion.10 = f32[4,128,128]{2,1,0:T(8,128)} fusion(bf16[512,4,128]{0,2,1:T(8,128)(2,1)S(1)} %bitcast.47, bf16[512,512]{1,0:T(8,128)(2,1)} %param.9), kind=kOutput, calls=%fused_computation.18 | convolution fusion | flops 67108864 | bytes 1310720 | tf_op jit(solution)/shard_map/thd,the->hde/dot_general | solution.py:48
  9.9 0.0 all-gather.9.cloned.1.call-update
  9.9 0.0 all-gather.5.cloned.1.call-start
  10.0 0.1 iota_compare_fusion
  10.1 51.8 %all-gather.9.cloned.1.call-done = f32[32,128,128]{2,1,0:T(8,128)} async-done(((f32[4,128,128]{2,1,0:T(8,128)}), f32[32,128,128]{2,1,0:T(8,128)}) %all-gather.9.cloned.1.call-update) | async-done | bytes 2097168 | tf_op jit(solution)/shard_map/all_gather | solution.py:11
  61.9 8.5 %while.14 = (s32[]{:T(128)}, f32[4,128,128]{2,1,0:T(8,128)S(1)}, s32[]{:T(128)}, f32[8,4,128,128]{3,2,1,0:T(8,128)}, s32[]{:T(128)}, /*index=5*/s32[]{:T(128)}) while((s32[]{:T(128)}, f32[4,128,128]{2,1,0:T(8,128)S(1)}, s32[]{:T(128)}, f32[8,4,128,128]{3,2,1,0:T(8,128)}, s32[]{:T(128)}, /*index=5*/s32[]{:T(128)}) %tuple.42), condition=%wide.region_1.2_spmd.clone, body=%wide.region_0.1_spmd.clone.sunk | while | flops 196612 | bytes 786525 | solution.py:19
  61.9 1.0 add_select_fusion.2
  62.9 1.0 add_select_fusion.2
  64.0 1.0 add_select_fusion.2
  65.1 1.0 add_select_fusion.2
  66.1 1.0 add_select_fusion.2
  67.2 1.0 add_select_fusion.2
  68.3 1.0 add_select_fusion.2
  69.3 1.0 add_select_fusion.2
  70.4 0.0 copy-done
  70.4 0.3 fusion.3
  70.7 2.4 %multiply_reduce_fusion = (f32[512]{0:T(512)S(1)}, f32[512,4,128]{0,2,1:T(8,128)S(1)}) fusion(f32[512,4,128]{0,2,1:T(8,128)S(1)} %fusion.3, bf16[512,4,128]{0,2,1:T(8,128)(2,1)S(1)} %bitcast.48, pred[512,512]{1,0:T(8,128)(4,1)S(1)} %iota_compare_fusion, bf16[512,512]{1,0:T(8,128)(2,1)} %param.9, bf16[512,512]{1,0:T(8,128)(2,1)S(1)} %copy-done), kind=kOutput, calls=%fused_computation.14 | convolution fusion | flops 540802560 | bytes 3934208 | tf_op jit(solution)/shard_map/hts,she->the/dot_general | solution.py:37
  73.2 0.0 copy-start.1
  73.2 0.3 copy.17
  73.5 0.7 copy-done.1
  74.2 1.1 fusion.8
  75.3 0.0 all-gather.5.cloned.1.call-update
  75.3 0.0 all-gather.7.cloned.1.call-start
  75.4 0.7 all-gather.7.cloned.1.call-update
  76.1 5.7 %psum.7 = f32[512]{0:T(512)S(1)} all-reduce(f32[512]{0:T(512)S(1)} %get-tuple-element.108), channel_id=1, replica_groups=mesh['seq'=8,'head'=4] {'head'}, use_global_device_ids=true, to_apply=%region_3.4 | all-reduce | flops 512 | bytes 4096 | tf_op jit(solution)/shard_map/psum | solution.py:60
  81.8 14.8 %all-gather.5.cloned.1.call-done = bf16[512,2048]{1,0:T(8,128)(2,1)} async-done(((bf16[512,512]{1,0:T(8,128)(2,1)}), bf16[512,2048]{1,0:T(8,128)(2,1)}) %all-gather.5.cloned.1.call-update) | async-done | bytes 2097168 | tf_op jit(solution)/shard_map/all_gather | solution.py:61
  96.6 75.0 %all-gather.7.cloned.1.call-done = bf16[2048,1024]{1,0:T(8,128)(2,1)} async-done(((bf16[256,1024]{1,0:T(8,128)(2,1)}), bf16[2048,1024]{1,0:T(8,128)(2,1)}) %all-gather.7.cloned.1.call-update) | async-done | bytes 4194320 | tf_op jit(solution)/shard_map/all_gather | solution.py:62
  171.6 6.1 %multiply_convert_fusion = bf16[512,1024]{1,0:T(8,128)(2,1)} fusion(bf16[512,2048]{1,0:T(8,128)(2,1)} %all-gather.5.cloned.1.call-done, bf16[2048,1024]{1,0:T(8,128)(2,1)} %all-gather.7.cloned.1.call-done, f32[512]{0:T(512)S(1)} %add_rsqrt_fusion), kind=kOutput, calls=%fused_computation.2 | convolution fusion | flops 2148532224 | bytes 7342080 | tf_op jit(solution)/shard_map/dot_general | solution.py:63
  (2 shorter events, 0.0 us)
Async XLA Ops:
  6.5 63.9 %copy-start = (bf16[512,512]{1,0:T(8,128)(2,1)S(1)}, bf16[512,512]{1,0:T(8,128)(2,1)}, u32[]{:S(2)}) copy-start(bf16[512,512]{1,0:T(8,128)(2,1)} %param.7) | copy-start | bytes 1572868
  6.5 55.3 %all-gather.9.cloned.1.call-start = ((), (), s32[]{:S(2)}) async-start(), calls=%async_computation.2 | async-start | bytes 2359296 | tf_op jit(solution)/shard_map/all_gather | solution.py:11
  9.9 86.7 %all-gather.5.cloned.1.call-start = ((), (), s32[]{:S(2)}) async-start(), calls=%async_computation | async-start | bytes 2621440 | tf_op jit(solution)/shard_map/all_gather | solution.py:61
  73.2 1.0 copy-start.1
  75.3 96.2 %all-gather.7.cloned.1.call-start = ((), (), s32[]{:S(2)}) async-start(), calls=%async_computation.1 | async-start | bytes 4718592 | tf_op jit(solution)/shard_map/all_gather | solution.py:62
Sparse Core Ops, SparseCore 0:
  10.0 51.7 all-gather.8
  75.5 21.0 all-gather.4
  98.7 72.7 all-gather.6
where the time goes:
time: 185 us; the launch traced here: 184 us
  waiting for transfers between devices  142 us (77%)
  between operations  13.2 us (7%)
  matrix products  10.9 us (6%)
  other arithmetic  9.53 us (5%)
  blocking collectives  5.67 us (3%)
  local copies, waits for them, and re-layouts  2.34 us (1%)
    all_gather x1, waiting for transfers between devices, per_device(): full_block = lax.all_gather(out_weight, 'seq', axis=0, tiled=True)  75 us
    all_gather x1, waiting for transfers between devices, carried_in(): everything = lax.all_gather(shard, axis)  51.8 us
    all_gather x1, waiting for transfers between devices, per_device(): features = lax.all_gather(hidden, 'head', axis=1, tiled=True)  14.8 us
    select_n x8, other arithmetic, turn(): return jnp.where(reached, new, before)  8.32 us
    dot_general x1, matrix products, per_device(): jnp.dot(features, full_block, preferred_element_type=jnp.float32)  6.12 us
    psum x1, blocking collectives, per_device(): total = lax.psum(squares, 'head')  5.67 us
  transfers between devices with their start and end apart: 3, of which 3 were waited for; matrix products, arithmetic and copies ran while one was open for 0% of the time, Pallas kernels for 0%

commit v1 on v0

--- a/solution.py
+++ b/solution.py
@@ -4,6 +4,18 @@
 from jax.sharding import PartitionSpec as P
 
 HD = 128
+
+
+def arrays_do(s0):
+    parts_n = lax.axis_size("head")
+    vals = []
+    for u in range(parts_n):
+        vals.append((u, (u + 1) % parts_n))
+    outer = [None] * parts_n
+    outer[parts_n - 1] = s0
+    for no in range(parts_n - 2, -1, -1):
+        outer[no] = lax.ppermute(outer[no + 1], "head", vals)
+    return jnp.roll(jnp.concatenate(outer, 1), (lax.axis_index("head") + 1) * s0.shape[1], 1)
 
 
 def carried_in(shard, axis, combine, identity):
@@ -58,7 +70,7 @@
     squares = jnp.sum(attn * attn, axis=1)
     hidden = (attn * jax.nn.silu(gate_input.astype(jnp.float32))).astype(jnp.bfloat16)
     total = lax.psum(squares, "head")
-    features = lax.all_gather(hidden, "head", axis=1, tiled=True)
+    features = arrays_do(hidden)
     full_block = lax.all_gather(out_weight, "seq", axis=0, tiled=True)
     projected = jnp.dot(features, full_block, preferred_element_type=jnp.float32)
     mean_square = total / features.shape[1]

time: 185 us -> 149 us (0.81)
  waiting for transfers between devices: 142 us -> 95.5 us
  local copies, waits for them, and re-layouts: 2.34 us -> 8.81 us
  blocking collectives: 5.67 us -> 9.54 us
    all_gather x1, waiting for transfers between devices: 75 us -> 26.5 us  [per_device(): full_block = lax.all_gather(out_weight, 'seq', axis=0, tiled=True)]
    ppermute x0 -> x3, waiting for transfers between devices: none -> 17.2 us  [arrays_do(): outer[no] = lax.ppermute(outer[no + 1], 'head', vals)]
    all_gather x1 -> x0, waiting for transfers between devices: 14.8 us -> none  [per_device(): features = lax.all_gather(hidden, 'head', axis=1, tiled=True)]
    unnamed x4 -> x9, local copies, waits for them, and re-layouts: 0.7 us -> 6.29 us
    psum x1, blocking collectives: 5.67 us -> 9.54 us  [per_device(): total = lax.psum(squares, 'head')]
  transfers between devices with their start and end apart: 3 -> 5, of which waited for: 3 -> 4; matrix products, arithmetic and copies ran while one was open for 0% -> 14% of each run, Pallas kernels for 0% -> 0%
where the time goes in v1:
time: 149 us; the launch traced here: 148 us
  waiting for transfers between devices  95.5 us (64%)
  between operations  13.5 us (9%)
  matrix products  10.9 us (7%)
  other arithmetic  9.79 us (7%)
  blocking collectives  9.54 us (6%)
  local copies, waits for them, and re-layouts  8.81 us (6%)
    all_gather x1, waiting for transfers between devices, carried_in(): everything = lax.all_gather(shard, axis)  51.1 us
    all_gather x1, waiting for transfers between devices, per_device(): full_block = lax.all_gather(out_weight, 'seq', axis=0, tiled=True)  26.5 us
    ppermute x3, waiting for transfers between devices, arrays_do(): outer[no] = lax.ppermute(outer[no + 1], 'head', vals)  17.2 us
    psum x1, blocking collectives, per_device(): total = lax.psum(squares, 'head')  9.54 us
    select_n x8, other arithmetic, turn(): return jnp.where(reached, new, before)  8.33 us
    unnamed x9, local copies, waits for them, and re-layouts  6.29 us
    dot_general x1, matrix products, per_device(): jnp.dot(features, full_block, preferred_element_type=jnp.float32)  6.12 us
  transfers between devices with their start and end apart: 5, of which 4 were waited for; matrix products, arithmetic and copies ran while one was open for 14% of the time, Pallas kernels for 0%

profile of v1, /device:TPU:0, one launch (start us, length us, event | category | flops | bytes accessed | tf_op | source)
XLA Modules:
  0.0 148.3 jit_solution(16035188707708265485)
XLA Ops:
  6.5 1.3 copy.19
  7.9 2.0 %fusion.14 = f32[4,128,128]{2,1,0:T(8,128)} fusion(bf16[512,4,128]{0,2,1:T(8,128)(2,1)S(1)} %bitcast.46, bf16[512,512]{1,0:T(8,128)(2,1)} %param.9), kind=kOutput, calls=%fused_computation.20 | convolution fusion | flops 67108864 | bytes 1310720 | tf_op jit(solution)/shard_map/thd,the->hde/dot_general | solution.py:60
  10.0 0.7 all-gather.4.cloned.1.call-update
  10.7 0.1 iota_compare_fusion
  10.8 51.1 %all-gather.6.cloned.1.call-done = f32[32,128,128]{2,1,0:T(8,128)} async-done(((f32[4,128,128]{2,1,0:T(8,128)}), f32[32,128,128]{2,1,0:T(8,128)}) %all-gather.6.cloned.1.call-update) | async-done | bytes 2097168 | tf_op jit(solution)/shard_map/all_gather | solution.py:23
  61.9 8.5 %while.14 = (s32[]{:T(128)}, f32[4,128,128]{2,1,0:T(8,128)S(1)}, s32[]{:T(128)}, f32[8,4,128,128]{3,2,1,0:T(8,128)}, s32[]{:T(128)}, /*index=5*/s32[]{:T(128)}) while((s32[]{:T(128)}, f32[4,128,128]{2,1,0:T(8,128)S(1)}, s32[]{:T(128)}, f32[8,4,128,128]{3,2,1,0:T(8,128)}, s32[]{:T(128)}, /*index=5*/s32[]{:T(128)}) %tuple.40), condition=%wide.region_1.2_spmd.clone, body=%wide.region_0.1_spmd.clone.sunk | while | flops 196612 | bytes 786525 | solution.py:31
  61.9 1.0 add_select_fusion.2
  62.9 1.0 add_select_fusion.2
  64.0 1.0 add_select_fusion.2
  65.1 1.0 add_select_fusion.2
  66.1 1.0 add_select_fusion.2
  67.2 1.0 add_select_fusion.2
  68.3 1.0 add_select_fusion.2
  69.3 1.1 add_select_fusion.2
  70.4 0.3 fusion.7
  70.8 2.4 %multiply_reduce_fusion = (f32[512]{0:T(512)S(1)}, f32[512,4,128]{0,2,1:T(8,128)S(1)}) fusion(f32[512,4,128]{0,2,1:T(8,128)S(1)} %fusion.7, bf16[512,4,128]{0,2,1:T(8,128)(2,1)S(1)} %bitcast.47, pred[512,512]{1,0:T(8,128)(4,1)S(1)} %iota_compare_fusion, bf16[512,512]{1,0:T(8,128)(2,1)} %param.9, bf16[512,512]{1,0:T(8,128)(2,1)S(1)} %copy-done), kind=kOutput, calls=%fused_computation.16 | convolution fusion | flops 540802560 | bytes 3934208 | tf_op jit(solution)/shard_map/hts,she->the/dot_general | solution.py:49
  73.2 0.3 copy.17
  73.5 1.4 fusion.12
  74.9 0.1 collective-permute-start
  75.0 8.6 %collective-permute-done = bf16[512,512]{1,0:T(8,128)(2,1)S(1)} collective-permute-done((bf16[512,512]{1,0:T(8,128)(2,1)S(1)}, bf16[512,512]{1,0:T(8,128)(2,1)S(1)}, u32[]{:S(2)}, u32[]{:S(2)}) %collective-permute-start) | collective-permute-done | bytes 524320 | tf_op jit(solution)/shard_map/ppermute | solution.py:17
  83.6 8.6 %collective-permute-done.1 = bf16[512,512]{1,0:T(8,128)(2,1)S(1)} collective-permute-done((bf16[512,512]{1,0:T(8,128)(2,1)S(1)}, bf16[512,512]{1,0:T(8,128)(2,1)S(1)}, u32[]{:S(2)}, u32[]{:S(2)}) %collective-permute-start.1) | collective-permute-done | bytes 524320 | tf_op jit(solution)/shard_map/ppermute | solution.py:17
  92.2 9.5 %psum.7 = f32[512]{0:T(512)S(1)} all-reduce(f32[512]{0:T(512)S(1)} %get-tuple-element.108), channel_id=1, replica_groups=mesh['seq'=8,'head'=4] {'head'}, use_global_device_ids=true, to_apply=%region_3.4 | all-reduce | flops 512 | bytes 4096 | tf_op jit(solution)/shard_map/psum | solution.py:72
  101.7 0.9 constant_dynamic-update-slice_fusion.7
  102.7 0.9 constant_dynamic-update-slice_fusion.6
  103.5 0.9 constant_dynamic-update-slice_fusion.5
  104.5 0.9 constant_dynamic-update-slice_fusion.4
  105.4 0.9 constant_dynamic-update-slice_fusion.3
  106.2 0.9 constant_dynamic-update-slice_fusion.2
  107.1 0.9 constant_dynamic-update-slice_fusion.1
  108.0 0.9 constant_dynamic-update-slice_fusion
  108.9 26.5 %all-gather.4.cloned.1.call-done = bf16[2048,1024]{1,0:T(8,128)(2,1)} async-done(((bf16[256,1024]{1,0:T(8,128)(2,1)}), bf16[2048,1024]{1,0:T(8,128)(2,1)}) %all-gather.4.cloned.1.call-update) | async-done | bytes 4194320 | tf_op jit(solution)/shard_map/all_gather | solution.py:74
  135.4 6.1 %multiply_convert_fusion = bf16[512,1024]{1,0:T(8,128)(2,1)} fusion(bf16[2048,1024]{1,0:T(8,128)(2,1)} %all-gather.4.cloned.1.call-done, bf16[512,4096]{1,0:T(8,128)(2,1)} %constant_dynamic-update-slice_fusion, s32[]{:T(128)S(6)} %select_n.40, f32[512]{0:T(512)S(1)} %add_rsqrt_fusion), kind=kOutput, calls=%fused_computation.2 | convolution fusion | flops 2148532224 | bytes 7342084 | tf_op jit(solution)/shard_map/dot_general | solution.py:75
  (10 shorter events, 0.1 us)
Async XLA Ops:
  6.5 63.9 %copy-start = (bf16[512,512]{1,0:T(8,128)(2,1)S(1)}, bf16[512,512]{1,0:T(8,128)(2,1)}, u32[]{:S(2)}) copy-start(bf16[512,512]{1,0:T(8,128)(2,1)} %param.7) | copy-start | bytes 1572868
  6.5 55.3 %all-gather.6.cloned.1.call-start = ((), (), s32[]{:S(2)}) async-start(), calls=%async_computation.1 | async-start | bytes 2359296 | tf_op jit(solution)/shard_map/all_gather | solution.py:23
  9.9 125.4 %all-gather.4.cloned.1.call-start = ((), (), s32[]{:S(2)}) async-start(), calls=%async_computation | async-start | bytes 4718592 | tf_op jit(solution)/shard_map/all_gather | solution.py:74
  74.9 8.7 %collective-permute-start = (bf16[512,512]{1,0:T(8,128)(2,1)S(1)}, bf16[512,512]{1,0:T(8,128)(2,1)S(1)}, u32[]{:S(2)}, u32[]{:S(2)}) collective-permute-start(bf16[512,512]{1,0:T(8,128)(2,1)S(1)} %fusion.12), channel_id=1, source_target_pairs={{0,1},{1,2},{2,3},{3,0},{4,5},{5,6},{6,7},{7,4},{8,9},{9,10},{10,1... | collective-permute-start | bytes 1572872 | tf_op jit(solution)/shard_map/ppermute | solution.py:17
  83.5 8.6 %collective-permute-start.1 = (bf16[512,512]{1,0:T(8,128)(2,1)S(1)}, bf16[512,512]{1,0:T(8,128)(2,1)S(1)}, u32[]{:S(2)}, u32[]{:S(2)}) collective-permute-start(bf16[512,512]{1,0:T(8,128)(2,1)S(1)} %collective-permute-done), channel_id=1, source_target_pairs={{0,1},{1,2},{2,3},{3,0},{4,5},{5,6},{6,7},{7,4},{8,9},{9,10},{10,1... | collective-permute-start | bytes 1572872 | tf_op jit(solution)/shard_map/ppermute | solution.py:17
  92.2 9.6 %collective-permute-start.2 = (bf16[512,512]{1,0:T(8,128)(2,1)S(1)}, bf16[512,512]{1,0:T(8,128)(2,1)S(1)}, u32[]{:S(2)}, u32[]{:S(2)}) collective-permute-start(bf16[512,512]{1,0:T(8,128)(2,1)S(1)} %collective-permute-done.1), channel_id=1, source_target_pairs={{0,1},{1,2},{2,3},{3,0},{4,5},{5,6},{6,7},{7,4},{8,9},{9,10},{10,1... | collective-permute-start | bytes 1572872 | tf_op jit(solution)/shard_map/ppermute | solution.py:17
Sparse Core Ops, SparseCore 0:
  10.0 51.7 all-gather.5
  64.0 71.3 all-gather.3
